TPU v7x, 32 devices: a 4x4x1 block of a 4x4x8 slice. The times are simulated.
32 devices in a mesh: dp: 1 (over z), cx: 4 (over y), cy: 8 (over x, core).
Axes of the slice: x: 4, y: 4, z: 1, core: 2. Of those that a mesh axis runs over, the one named last changes fastest.
The devices are a block of a 4x4x8 slice.
Arguments:
- x: bfloat16 [1, 2048, 3072], P('dp', ('cx', 'cy'))
- w_qkv: bfloat16 [3072, 9216], replicated
- w_o: bfloat16 [48, 64, 3072], replicated
Outputs:
- output: bfloat16 [1, 2048, 3072], P('dp', ('cx', 'cy'))
All inputs are finite; a program needn't handle non-finite values.
Results may differ from a plain program's by a relative error of at most 0.0080538.
Values are sent between devices in bfloat16 or wider.
A program may use at most 768 MiB of HBM per device.

v0:
```python
import jax
import jax.numpy as jnp
from jax import lax
from jax.sharding import PartitionSpec as P


def solution(mesh):
    def attend_local(x_blk, w_qkv, w_o):
        num_heads, head_dim = w_o.shape[0], w_o.shape[1]
        tok_rows = x_blk.shape[1]
        inv_sqrt = head_dim ** -0.5
        qkv_rows = jnp.dot(x_blk[0], w_qkv, preferred_element_type=jnp.float32).astype(jnp.bfloat16)
        qkv_rows = lax.all_to_all(qkv_rows.reshape(tok_rows, 3, num_heads, head_dim), "cy", 2, 0, tiled=True)
        kv_all = lax.all_gather(qkv_rows[:, 1:], "cx", axis=0, tiled=True)
        logits = jnp.einsum("qhd,khd->hqk", qkv_rows[:, 0], kv_all[:, 0], preferred_element_type=jnp.float32) * inv_sqrt
        row_max = jnp.max(logits, axis=-1, keepdims=True)
        weights = jnp.exp(logits - row_max)
        row_sum = jnp.sum(weights, axis=-1, keepdims=True)
        attn_rows = jnp.einsum("hqk,khd->qhd", weights.astype(jnp.bfloat16), kv_all[:, 1], preferred_element_type=jnp.float32)
        attn_rows = (attn_rows / jnp.transpose(row_sum, (1, 0, 2))).astype(jnp.bfloat16)
        attn_rows = lax.all_to_all(attn_rows, "cy", 0, 1, tiled=True)
        result = jnp.einsum("thd,hdc->tc", attn_rows, w_o, preferred_element_type=jnp.float32)
        return result.astype(jnp.bfloat16)[None]

    return jax.shard_map(attend_local, mesh=mesh, in_specs=(P("dp", ("cx", "cy"), None), P(None, None), P(None, None, None)), out_specs=P("dp", ("cx", "cy"), None), check_vma=False)
```

profile of v0, /device:TPU:97, one launch (start us, length us, event | category | flops | bytes accessed | tf_op | source)
XLA Modules:
  0.0 169.3 jit_solution(540058333097664208)
XLA Ops:
  6.5 0.0 copy-start
  6.6 0.0 all-gather.2.cloned.1.call-start
  6.6 1.0 copy-done
  7.5 21.9 %convolution_convert_fusion = bf16[64,9216]{1,0:T(8,128)(2,1)} fusion(bf16[3072,9216]{1,0:T(8,128)(2,1)} %param.4, bf16[1,64,3072]{2,1,0:T(8,128)(2,1)S(1)} %copy-done), kind=kOutput, calls=%fused_computation.5 | convolution fusion | flops 3624468480 | bytes 58195968 | tf_op jit(solution)/shard_map/dot_general | solution.py:12
  29.4 3.0 %reshape.4 = bf16[64,3,48,64]{3,2,1,0:T(8,128)(2,1)S(1)} reshape(bf16[64,9216]{1,0:T(8,128)(2,1)} %convolution_convert_fusion) | data formatting | bytes 2359296 | tf_op jit(solution)/shard_map/reshape | solution.py:13
  32.5 2.0 %copy.16 = bf16[64,3,48,64]{3,0,1,2:T(8,128)(2,1)} copy(bf16[64,3,48,64]{3,2,1,0:T(8,128)(2,1)S(1)} %reshape.4) | data formatting | bytes 2359296 | tf_op jit(solution)/shard_map/reshape | solution.py:13
  34.5 3.5 %reshape.6 = bf16[8,2,36864]{2,1,0:T(2,128)(2,1)S(1)} reshape(bf16[48,3,64,64]{3,2,1,0:T(8,128)(2,1)} %bitcast.59) | data formatting | bytes 2359296
  38.0 22.3 %all_to_all.36 = bf16[8,2,36864]{2,1,0:T(2,128)(2,1)} all-to-all(bf16[8,2,36864]{2,1,0:T(2,128)(2,1)S(1)} %reshape.6), channel_id=1, replica_groups=mesh['dp'=1,'cx'=4,'cy'=8] {'cy'}, dimensions={0} | all-to-all | bytes 2359296 | tf_op jit(solution)/shard_map/all_to_all | solution.py:13
  60.3 3.3 %reshape.7 = bf16[48,3,64,64]{3,2,1,0:T(8,128)(2,1)S(1)} reshape(bf16[8,2,36864]{2,1,0:T(2,128)(2,1)} %all_to_all.36) | data formatting | bytes 2359296
  63.6 2.7 %copy.11 = bf16[8,64,3,6,64]{1,0,4,3,2:T(8,128)(2,1)} copy(bf16[8,64,3,6,64]{4,1,2,3,0:T(8,128)(2,1)S(1)} %bitcast.60) | data formatting | bytes 2359296 | tf_op jit(solution)/shard_map/all_to_all | solution.py:13
  66.3 3.4 %all_to_all.29 = bf16[512,3,6,64]{0,3,2,1:T(8,128)(2,1)S(1)} reshape(bf16[8,64,3,6,64]{1,0,4,3,2:T(8,128)(2,1)} %copy.11) | data formatting | bytes 2359296 | tf_op jit(solution)/shard_map/all_to_all | solution.py:13
  69.7 0.0 copy-start.3
  69.7 1.1 slice.16
  70.8 0.1 all-gather.2.cloned.1.call-update
  70.9 0.1 copy-done.3
  71.0 37.8 %all-gather.2.cloned.1.call-done = bf16[2048,2,6,64]{0,3,2,1:T(8,128)(2,1)} async-done(((bf16[512,2,6,64]{0,3,2,1:T(8,128)(2,1)}), bf16[2048,2,6,64]{0,3,2,1:T(8,128)(2,1)}) %all-gather.2.cloned.1.call-update) | async-done | bytes 3145744 | tf_op jit(solution)/shard_map/all_gather | solution.py:14
  108.7 5.1 %multiply_reduce_fusion = (f32[6,512]{1,0:T(8,128)S(1)}, f32[6,512,2048]{2,1,0:T(8,128)S(1)}) fusion(bf16[2048,2,6,64]{0,3,2,1:T(8,128)(2,1)} %all-gather.2.cloned.1.call-done, bf16[512,3,6,64]{0,3,2,1:T(8,128)(2,1)} %copy-done.3), kind=kOutput, calls=%fused_computation.1 | convolution fusion | flops 817886208 | bytes 27144192 | tf_op jit(solution)/shard_map/qhd,khd->hqk/dot_general | solution.py:15
  113.8 0.0 copy-start.2
  113.8 8.3 %copy-done.2 = f32[6,512,2048]{2,1,0:T(8,128)} copy-done((f32[6,512,2048]{2,1,0:T(8,128)}, f32[6,512,2048]{2,1,0:T(8,128)S(1)}, u32[]{:S(2)}) %copy-start.2) | copy-done | bytes 25165848
  122.1 4.9 %fusion = f32[6,512]{1,0:T(8,128)S(1)} fusion(f32[6,512,2048]{2,1,0:T(8,128)S(1)} %get-tuple-element.6, f32[6,512]{1,0:T(8,128)S(1)} %get-tuple-element.5), kind=kLoop, calls=%fused_computation.2 | loop fusion | flops 18871296 | bytes 25190400 | tf_op jit(solution)/shard_map/reduce_sum | solution.py:18
  127.0 0.0 copy-start.1
  127.0 11.1 %fusion.13 = bf16[512,6,64]{0,2,1:T(8,128)(2,1)S(1)} fusion(f32[6,512,2048]{2,1,0:T(8,128)} %copy-done.2, f32[6,512]{1,0:T(8,128)S(1)} %get-tuple-element.5, bf16[2048,2,6,64]{0,3,2,1:T(8,128)(2,1)} %all-gather.2.cloned.1.call-done, f32[512,6]{0,1:T(8,128)S(1)} %bitcast.63), kind=kOutput, calls=%fused_computation.14 | convolution fusion | flops 824573952 | bytes 27156480 | tf_op jit(solution)/shard_map/hqk,khd->qhd/dot_general | solution.py:19
  138.1 0.8 copy.12
  138.9 0.7 reshape.8
  139.6 13.0 %all_to_all.37 = bf16[8,2,12288]{2,1,0:T(2,128)(2,1)S(1)} all-to-all(bf16[8,2,12288]{2,1,0:T(2,128)(2,1)S(1)} %reshape.8), channel_id=1, replica_groups=mesh['dp'=1,'cx'=4,'cy'=8] {'cy'}, dimensions={0} | all-to-all | bytes 786432 | tf_op jit(solution)/shard_map/all_to_all | solution.py:21
  152.6 0.6 reshape.9
  153.2 0.2 copy.13
  153.4 9.0 %fusion.5 = bf16[1,64,3072]{2,1,0:T(8,128)(2,1)} fusion(bf16[64,48,64]{2,0,1:T(8,128)(2,1)S(1)} %bitcast.62, bf16[48,64,3072]{2,1,0:T(8,128)(2,1)} %param.5), kind=kOutput, calls=%fused_computation.8 | convolution fusion | flops 1208156160 | bytes 19660800 | tf_op jit(solution)/shard_map/thd,hdc->tc/dot_general | solution.py:22
  162.4 0.0 copy-done.1
Async XLA Ops:
  6.5 1.0 copy-start
  6.6 102.2 %all-gather.2.cloned.1.call-start = ((), (), s32[]{:S(2)}) async-start(), calls=%async_computation.2 | async-start | bytes 3932160 | tf_op jit(solution)/shard_map/all_gather | solution.py:14
  69.7 1.3 copy-start.3
  113.8 8.3 %copy-start.2 = (f32[6,512,2048]{2,1,0:T(8,128)}, f32[6,512,2048]{2,1,0:T(8,128)S(1)}, u32[]{:S(2)}) copy-start(f32[6,512,2048]{2,1,0:T(8,128)S(1)} %get-tuple-element.6) | copy-start | bytes 75497472
  127.0 35.4 %copy-start.1 = (bf16[1,64,3072]{2,1,0:T(8,128)(2,1)S(1)}, bf16[1,64,3072]{2,1,0:T(8,128)(2,1)}, u32[]{:S(2)}) copy-start(bf16[1,64,3072]{2,1,0:T(8,128)(2,1)} %param.3) | copy-start | bytes 1179652
Sparse Core Ops, SparseCore 0:
  71.0 37.6 all-gather.1
where the time goes:
time: 170 us; the launch traced here: 169 us
  matrix products  47 us (28%)
  waiting for transfers between devices  37.8 us (22%)
  blocking collectives  35.3 us (21%)
  local copies, waits for them, and re-layouts  30.7 us (18%)
  between operations  13.5 us (8%)
  other arithmetic  4.88 us (3%)
    all_gather x1, waiting for transfers between devices, attend_local(): kv_all = lax.all_gather(qkv_rows[:, 1:], 'cx', axis=0, tiled=True)  37.8 us
    all_to_all x1, blocking collectives, attend_local(): lax.all_to_all(qkv_rows.reshape(tok_rows, 3, num_heads, head_dim), 'cy',...  22.3 us
    dot_general x1, matrix products, attend_local(): jnp.dot(x_blk[0], w_qkv, preferred_element_type=jnp.float32)  21.9 us
    unnamed x12, local copies, waits for them, and re-layouts  17.5 us
    all_to_all x1, blocking collectives, attend_local(): attn_rows = lax.all_to_all(attn_rows, 'cy', 0, 1, tiled=True)  13 us
    dot_general x1, matrix products, attend_local(): jnp.einsum('hqk,khd->qhd', weights.astype(jnp.bfloat16), kv_all[:, 1], pr...  11.1 us
    dot_general x1, matrix products, attend_local(): jnp.einsum('thd,hdc->tc', attn_rows, w_o, preferred_element_type=jnp.floa...  8.97 us
    all_to_all x2, local copies, waits for them, and re-layouts, attend_local(): lax.all_to_all(qkv_rows.reshape(tok_rows, 3, num_heads, head_dim), 'cy',...  6.12 us
  transfers between devices with their start and end apart: 1, of which 1 were waited for; matrix products, arithmetic and copies ran while one was open for 0% of the time, Pallas kernels for 0%

commit v1 on v0

v1 whole, which is shorter than its diff:
```python
import functools

import jax
import jax.numpy as jnp
from jax import lax
from jax.experimental import pallas as pl
from jax.experimental.pallas import tpu as pltpu
from jax.sharding import PartitionSpec as P

MESH = pl.DeviceIdType.MESH
BF16, F32 = jnp.bfloat16, jnp.float32
LOG2E = 1.4426950408889634


def kernel(cfg, x_ref, w_ref, wo_ref, y_ref, xv, wv, wov, stage, buf, ostage, obuf, acc,
           x_sem, w_sem, wo_sem, xs_sem, xr_sem, qs_sem, qr_sem, fs_sem, fr_sem, os_sem, or_sem):
    n_cx, n_cy, chips, chunks, heads, hd = cfg
    row_chips = n_cy // 2
    half = chips // 2
    rows = x_ref.shape[0]
    width = x_ref.shape[1]
    kv_rows = 2 * rows
    span = half * hd
    scale = hd ** -0.5 * LOG2E

    i = lax.axis_index("cx")
    j = lax.axis_index("cy")
    xx = j // 2
    c = lax.rem(j, 2)
    e = i * row_chips + xx
    par = lax.rem(e, 2)

    def dev(chip, core):
        return {"cx": chip // row_chips, "cy": lax.rem(chip, row_chips) * 2 + core}

    my_rows = pl.ds(pl.multiple_of(c * rows, rows), rows)
    x_in = pltpu.make_async_copy(x_ref, xv.at[my_rows], x_sem)
    x_in.start()

    def w_copy(s, t):
        col = pl.multiple_of((t * heads + s * chips) * hd + c * span, 128)
        return pltpu.make_async_copy(w_ref.at[:, pl.ds(col, span)], wv.at[3 * s + t], w_sem.at[3 * s + t])

    def wo_copy(s):
        part = pl.ds(s * chips * hd, chips * hd)
        return pltpu.make_async_copy(wo_ref.at[part], wov.at[part], wo_sem.at[s])

    for s in range(chunks):
        for t in range(3):
            w_copy(s, t).start()
    for s in range(chunks):
        wo_copy(s).start()

    n_dev = n_cx * n_cy
    barrier = pltpu.get_barrier_semaphore()

    def greet(k, _):
        other = lax.rem(i * n_cy + j + k, n_dev)
        pl.semaphore_signal(barrier, inc=1, device_id={"cx": other // n_cy, "cy": lax.rem(other, n_cy)},
                            device_id_type=MESH)
        return 0

    lax.fori_loop(1, n_dev, greet, 0)
    pl.semaphore_wait(barrier, n_dev - 1)

    x_in.wait()
    x_swap = pltpu.make_async_remote_copy(xv.at[my_rows], xv.at[my_rows], xs_sem, xr_sem,
                                          device_id=dev(e, 1 - c), device_id_type=MESH)
    x_swap.start()
    x_swap.wait()

    lane = lax.broadcasted_iota(jnp.int32, (kv_rows, 128), 1)
    low = lane < hd
    low_q = low[:rows]
    low_o = low[:rows // 2]

    def qkv_send(s, k):
        d = c * half + k
        return pltpu.make_async_remote_copy(stage.at[s, k], buf.at[s, e], qs_sem.at[s, k], qr_sem.at[s, e // 2],
                                            device_id=dev(d, par), device_id_type=MESH)

    def project(s):
        parts = []
        for t in range(3):
            w_copy(s, t).wait()
            parts.append(jnp.dot(xv[...], wv[3 * s + t], preferred_element_type=F32))
        for p in range(half // 2):
            sl = slice(128 * p, 128 * p + 128)
            q, k, v = (a[:, sl] for a in parts)
            q_lo, q_hi = q[:rows], q[rows:]
            stage[s, 2 * p, 0:rows] = jnp.where(low_q, q_lo, pltpu.roll(q_hi, hd, 1)).astype(BF16)
            stage[s, 2 * p + 1, 0:rows] = jnp.where(low_q, pltpu.roll(q_lo, hd, 1), q_hi).astype(BF16)
            stage[s, 2 * p, rows:] = jnp.where(low, k, pltpu.roll(v, hd, 1)).astype(BF16)
            stage[s, 2 * p + 1, rows:] = jnp.where(low, pltpu.roll(k, hd, 1), v).astype(BF16)

        def send(n, _):
            dx = lax.rem(n // 2 + 1 + xx, row_chips)
            k = lax.rem(n, 2) * row_chips + dx
            mine = jnp.logical_and(c * half + k == e, par == c)

            @pl.when(mine)
            def _():
                buf[s, e] = stage[s, k]

            @pl.when(jnp.logical_not(mine))
            def _():
                qkv_send(s, k).start()
            return 0

        lax.fori_loop(0, half, send, 0)

    def sent(s):
        def one(k, _):
            @pl.when(jnp.logical_not(jnp.logical_and(c * half + k == e, par == c)))
            def _():
                qkv_send(s, k).wait_send()
            return 0

        lax.fori_loop(0, half, one, 0)

    def fwd(s, n, core):
        part = buf.at[s, 2 * n + core, pl.ds(rows, kv_rows)]
        return pltpu.make_async_remote_copy(part, part, fs_sem.at[s, n], fr_sem.at[s, n],
                                            device_id=dev(e, 1 - c), device_id_type=MESH)

    def forward(s):
        def one(n, _):
            src = 2 * n + c
            local = jnp.logical_and(src == e, e // half == c)

            @pl.when(jnp.logical_not(local))
            def _():
                pltpu.make_async_remote_copy(buf.at[s, src], buf.at[s, src], qs_sem.at[s, 0], qr_sem.at[s, n],
                                             device_id=dev(e, 1 - c), device_id_type=MESH).wait_recv()
            fwd(s, n, c).start()
            return 0

        lax.fori_loop(0, half, one, 0)

    def o_send(s, n, core):
        q_chip = 2 * n + c
        return pltpu.make_async_remote_copy(ostage.at[s, 2 * n + core], obuf.at[s, e], os_sem.at[s, 2 * n + core],
                                            or_sem.at[s, e], device_id=dev(q_chip, core), device_id_type=MESH)

    def attend(s):
        def got(n, _):
            fwd(s, n, 1 - c).wait_recv()
            return 0

        lax.fori_loop(0, half, got, 0)

        def block(b, _):
            qs = []
            for u in range(2):
                qq = buf[s, 2 * (2 * b + u) + c, 0:rows].astype(F32)
                qs.append(jnp.where(low_q, qq, 0.0).astype(BF16))
                qs.append(jnp.where(low_q, pltpu.roll(qq, hd, 1), 0.0).astype(BF16))
            q = jnp.concatenate(qs, axis=0)
            kv = jnp.concatenate([buf[s, n, rows:] for n in range(chips)], axis=0)
            logits = lax.dot_general(q, kv, (((1,), (1,)), ((), ())), preferred_element_type=F32)
            m = jnp.max(logits, axis=1, keepdims=True)
            w = jnp.exp2((logits - m) * scale)
            den = jnp.sum(w, axis=1, keepdims=True)
            o = jnp.dot(w.astype(BF16), kv, preferred_element_type=F32) / den
            hr = rows // 2
            for u in range(4):
                top, bot = o[u * rows:u * rows + hr], o[u * rows + hr:(u + 1) * rows]
                ostage[s, 4 * b + u] = jnp.where(low_o, pltpu.roll(top, hd, 1), bot).astype(BF16)
            for u in range(4):
                n, core = 2 * b + u // 2, u % 2
                mine = jnp.logical_and(2 * n + c == e, c == core)

                @pl.when(mine)
                def _():
                    obuf[s, e] = ostage[s, 4 * b + u]

                @pl.when(jnp.logical_not(mine))
                def _():
                    o_send(s, n, core).start()
            return 0

        lax.fori_loop(0, half // 2, block, 0)

    def o_sent(s):
        def one(n, _):
            for core in range(2):
                @pl.when(jnp.logical_not(jnp.logical_and(2 * n + c == e, c == core)))
                def _():
                    o_send(s, n, core).wait_send()
            return 0

        lax.fori_loop(0, half, one, 0)

    def output(s):
        def got(d, _):
            @pl.when(jnp.logical_not(jnp.logical_and(d == e, par == c)))
            def _():
                pltpu.make_async_remote_copy(obuf.at[s, d], obuf.at[s, d], os_sem.at[s, 0], or_sem.at[s, d],
                                             device_id=dev(e, 1 - c), device_id_type=MESH).wait_recv()
            return 0

        lax.fori_loop(0, chips, got, 0)
        wo_copy(s).wait()
        tiles = []
        for p in range(half):
            a, b = obuf[s, 2 * p].astype(F32), obuf[s, 2 * p + 1].astype(F32)
            top = jnp.where(low_o, a, pltpu.roll(b, hd, 1))
            bot = jnp.where(low_o, pltpu.roll(a, hd, 1), b)
            tiles.append(jnp.concatenate([top, bot], axis=0).astype(BF16))
        o = jnp.concatenate(tiles, axis=1)
        part = jnp.dot(o, wov[s * chips * hd:(s + 1) * chips * hd], preferred_element_type=F32)
        if s == 0:
            acc[...] = part
        elif s < chunks - 1:
            acc[...] += part
        else:
            y_ref[...] = (acc[...] + part).astype(BF16)

    for s in range(chunks):
        project(s)
    forward(0)
    attend(0)
    forward(1)
    attend(1)
    forward(2)
    output(0)
    attend(2)
    output(1)
    output(2)
    for s in range(chunks):
        sent(s)
        o_sent(s)

        def one(n, _):
            fwd(s, n, c).wait_send()
            return 0

        lax.fori_loop(0, half, one, 0)


def solution(mesh):
    n_cx, n_cy = mesh.shape["cx"], mesh.shape["cy"]
    chips = n_cx * n_cy // 2

    def attend_local(x_blk, w_qkv, w_o):
        heads, hd, width = w_o.shape
        rows = x_blk.shape[1]
        chunks = heads // chips
        half = chips // 2
        dma, vm = pltpu.SemaphoreType.DMA, pltpu.VMEM
        any_ = pl.BlockSpec(memory_space=pl.ANY)
        y = pl.pallas_call(
            functools.partial(kernel, (n_cx, n_cy, chips, chunks, heads, hd)),
            out_shape=jax.ShapeDtypeStruct((rows, width), BF16),
            in_specs=[any_, any_, any_],
            out_specs=pl.BlockSpec(memory_space=pltpu.VMEM),
            scratch_shapes=[
                vm((2 * rows, width), BF16),
                vm((3 * chunks, width, half * hd), BF16),
                vm((heads * hd, width), BF16),
                vm((chunks, half, 3 * rows, 128), BF16),
                vm((chunks, chips, 3 * rows, 128), BF16),
                vm((chunks, chips, rows // 2, 128), BF16),
                vm((chunks, chips, rows // 2, 128), BF16),
                vm((rows, width), F32),
                dma, dma((3 * chunks,)), dma((chunks,)), dma, dma,
                dma((chunks, half)), dma((chunks, half)),
                dma((chunks, half)), dma((chunks, half)),
                dma((chunks, chips)), dma((chunks, chips)),
            ],
            compiler_params=pltpu.CompilerParams(
                collective_id=0, has_side_effects=True, vmem_limit_bytes=63 * 2 ** 20),
        )(x_blk[0], w_qkv, w_o.reshape(heads * hd, width))
        return y[None]

    return jax.shard_map(
        attend_local, mesh=mesh,
        in_specs=(P("dp", ("cx", "cy"), None), P(None, None), P(None, None, None)),
        out_specs=P("dp", ("cx", "cy"), None), check_vma=False)
```

time: 170 us -> 58.1 us (0.34)
  Pallas kernels: 0 us -> 56.2 us
  matrix products: 47 us -> 0 us
  waiting for transfers between devices: 37.8 us -> 0 us
  blocking collectives: 35.3 us -> 0 us
  local copies, waits for them, and re-layouts: 30.7 us -> 1.77 us
  between operations: 13.5 us -> 0.01 us
  other arithmetic: 4.88 us -> 0 us
    pallas_call x0 -> x1, Pallas kernels: none -> 56.2 us  [attend_local(): pl.pallas_call(functools.partial(kernel, (n_cx, n_cy, chips, chunks, head...]
    dot_general x4 -> x0, matrix products: 47 us -> none  [the longest x1 21.9 us: attend_local(): jnp.dot(x_blk[0], w_qkv, preferred_element_type=jnp.float32)]
    all_gather x1 -> x0, waiting for transfers between devices: 37.8 us -> none  [attend_local(): kv_all = lax.all_gather(qkv_rows[:, 1:], 'cx', axis=0, tiled=True)]
    all_to_all x2 -> x0, blocking collectives: 35.3 us -> none  [the longest x1 22.3 us: attend_local(): lax.all_to_all(qkv_rows.reshape(tok_rows, 3, num_heads, head_dim), 'cy',...]
    unnamed x12 -> x1, local copies, waits for them, and re-layouts: 17.5 us -> 1.77 us
    all_to_all x3 -> x0, local copies, waits for them, and re-layouts: 6.32 us -> none  [the longest x2 6.12 us: attend_local(): lax.all_to_all(qkv_rows.reshape(tok_rows, 3, num_heads, head_dim), 'cy',...]
    reshape x2 -> x0, local copies, waits for them, and re-layouts: 5.06 us -> none  [attend_local(): qkv_rows.reshape(tok_rows, 3, num_heads, head_dim)]
    reduce_sum x1 -> x0, other arithmetic: 4.88 us -> none  [attend_local(): row_sum = jnp.sum(weights, axis=-1, keepdims=True)]
  transfers between devices with their start and end apart: 1 -> 0, of which waited for: 1 -> 0; matrix products, arithmetic and copies ran while one was open for 0% -> 0% of each run, Pallas kernels for 0% -> 0%
where the time goes in v1:
time: 58.1 us; the launch traced here: 57.9 us
  Pallas kernels  56.2 us (97%)
  local copies, waits for them, and re-layouts  1.77 us (3%)
    pallas_call x1, Pallas kernels, attend_local(): pl.pallas_call(functools.partial(kernel, (n_cx, n_cy, chips, chunks, head...  56.2 us
    unnamed x1, local copies, waits for them, and re-layouts  1.77 us

profile of v1, /device:TPU:97, one launch (start us, length us, event | category | flops | bytes accessed | tf_op | source)
XLA Modules:
  0.0 57.9 jit_solution(13377074209343115480)
XLA Ops:
  0.0 56.2 %shard_map.37 = bf16[64,3072]{1,0:T(8,128)(2,1)} custom-call(bf16[64,3072]{1,0:T(8,128)(2,1)} %bitcast.5, bf16[3072,9216]{1,0:T(8,128)(2,1)} %w_ref.1, bf16[3072,3072]{1,0:T(8,128)(2,1)} %bitcast.3), custom_call_target="tpu_custom_call" | custom-call | tf_op jit(solution)/shard_map/pallas_call | solution.py:252
  56.2 1.8 %copy.5 = bf16[1,64,3072]{2,1,0:T(8,128)(2,1)} copy(bf16[1,64,3072]{2,1,0:T(8,128)(2,1)} %bitcast.4) | data formatting | bytes 786432

commit v2 on v1

--- a/solution.py
+++ b/solution.py
@@ -45,11 +45,8 @@
         part = pl.ds(s * chips * hd, chips * hd)
         return pltpu.make_async_copy(wo_ref.at[part], wov.at[part], wo_sem.at[s])
 
-    for s in range(chunks):
-        for t in range(3):
-            w_copy(s, t).start()
-    for s in range(chunks):
-        wo_copy(s).start()
+    for t in range(3):
+        w_copy(0, t).start()
 
     n_dev = n_cx * n_cy
     barrier = pltpu.get_barrier_semaphore()
@@ -83,6 +80,10 @@
         parts = []
         for t in range(3):
             w_copy(s, t).wait()
+            if s + 1 < chunks:
+                w_copy(s + 1, t).start()
+            else:
+                wo_copy(t).start()
             parts.append(jnp.dot(xv[...], wv[3 * s + t], preferred_element_type=F32))
         for p in range(half // 2):
             sl = slice(128 * p, 128 * p + 128)

time: 58.1 us -> 48.4 us (0.83)
  Pallas kernels: 56.2 us -> 46 us
    pallas_call x1, Pallas kernels: 56.2 us -> 46 us  [attend_local(): pl.pallas_call(functools.partial(kernel, (n_cx, n_cy, chips, chunks, head...]
where the time goes in v2:
time: 48.4 us; the launch traced here: 47.8 us
  Pallas kernels  46 us (95%)
  local copies, waits for them, and re-layouts  1.77 us (4%)
    pallas_call x1, Pallas kernels, attend_local(): pl.pallas_call(functools.partial(kernel, (n_cx, n_cy, chips, chunks, head...  46 us
    unnamed x1, local copies, waits for them, and re-layouts  1.77 us

profile of v2, /device:TPU:97, one launch (start us, length us, event | category | flops | bytes accessed | tf_op | source)
XLA Modules:
  0.0 47.8 jit_solution(5149812395247468089)
XLA Ops:
  0.0 46.0 %shard_map.37 = bf16[64,3072]{1,0:T(8,128)(2,1)} custom-call(bf16[64,3072]{1,0:T(8,128)(2,1)} %bitcast.5, bf16[3072,9216]{1,0:T(8,128)(2,1)} %w_ref.1, bf16[3072,3072]{1,0:T(8,128)(2,1)} %bitcast.3), custom_call_target="tpu_custom_call" | custom-call | tf_op jit(solution)/shard_map/pallas_call | solution.py:253
  46.0 1.8 %copy.5 = bf16[1,64,3072]{2,1,0:T(8,128)(2,1)} copy(bf16[1,64,3072]{2,1,0:T(8,128)(2,1)} %bitcast.4) | data formatting | bytes 786432

commit v3 on v0

v3 whole, which is shorter than its diff:
```python
import functools

import jax
import jax.numpy as jnp
from jax import lax
from jax.experimental import pallas as pl
from jax.experimental.pallas import tpu as pltpu
from jax.sharding import PartitionSpec as P

MESH = pl.DeviceIdType.MESH
BF16, F32 = jnp.bfloat16, jnp.float32
LOG2E = 1.4426950408889634
GROUPS = 2
BLOCKS = 2


def both(a, b):
    return jnp.logical_and(a, b)


def kernel(cfg, x_ref, w_ref, wo_ref, y_ref, xv, wv, stage, buf, ostage, obuf, acc,
           x_sem, w_sem, wo_sem, xs_sem, xr_sem, qs_sem, qr_sem, fs_sem, fr_sem, os_sem, or_sem):
    n_cx, n_cy, chips, chunks, heads, hd = cfg
    row_chips = n_cy // 2
    half = chips // 2
    rows, width = x_ref.shape
    kv_rows = 2 * rows
    span = half * hd
    scale = hd ** -0.5 * LOG2E
    group = half // GROUPS
    steps = chunks * GROUPS
    o_rows = chips * hd
    o_cols = group * hd
    o_parts = width // o_cols
    per = width // o_rows

    i = lax.axis_index("cx")
    j = lax.axis_index("cy")
    xx = lax.div(j, 2)
    c = lax.rem(j, 2)
    e = i * row_chips + xx
    par = lax.rem(e, 2)
    pair = lax.div(e, 2)

    def dev(chip, core):
        return {"cx": lax.div(chip, row_chips), "cy": lax.rem(chip, row_chips) * 2 + core}

    my_rows = pl.ds(pl.multiple_of(c * rows, rows), rows)
    x_in = pltpu.make_async_copy(x_ref, xv.at[my_rows], x_sem)
    x_in.start()

    def step(n):
        return lax.div(n, GROUPS), c * half + lax.rem(lax.rem(n, GROUPS) + i, GROUPS) * group

    def w_copy(n, t):
        s, first = step(n)
        col = pl.multiple_of((t * heads + s * chips + first) * hd, 128)
        return pltpu.make_async_copy(w_ref.at[:, pl.ds(col, group * hd)], wv.at[3 * n + t], w_sem.at[n])

    def wo_part(s, n):
        m = s * o_parts + n
        return wv.at[lax.div(m, per), pl.ds(pl.multiple_of(lax.rem(m, per) * o_rows, o_rows), o_rows)]

    def wo_copy(s, n):
        src = wo_ref.at[pl.ds(pl.multiple_of(s * o_rows, o_rows), o_rows), pl.ds(n * o_cols, o_cols)]
        return pltpu.make_async_copy(src, wo_part(s, n), wo_sem.at[s])

    def arrived(ref, sem):
        pltpu.make_async_copy(ref, ref, sem).wait()

    for t in range(3):
        w_copy(0, t).start()

    n_dev = n_cx * n_cy
    barrier = pltpu.get_barrier_semaphore()

    def greet(k, _):
        other = lax.rem(i * n_cy + j + k, n_dev)
        pl.semaphore_signal(barrier, inc=1, device_id={"cx": lax.div(other, n_cy), "cy": lax.rem(other, n_cy)},
                            device_id_type=MESH)
        return 0

    lax.fori_loop(1, n_dev, greet, 0)
    for t in range(3):
        w_copy(1, t).start()
    pl.semaphore_wait(barrier, n_dev - 1)

    x_in.wait()
    for t in range(3):
        w_copy(2, t).start()
    x_swap = pltpu.make_async_remote_copy(xv.at[my_rows], xv.at[my_rows], xs_sem, xr_sem,
                                          device_id=dev(e, 1 - c), device_id_type=MESH)
    x_swap.start()
    x_swap.wait()

    low = lax.broadcasted_iota(jnp.int32, (kv_rows, 128), 1) < hd
    low_q = low[:rows]
    low_o = low[:rows // 2]

    def qkv_send(n, kk):
        s, first = step(n)
        return pltpu.make_async_remote_copy(stage.at[s, slot(n) + kk], buf.at[s, par, pair], qs_sem.at[s], qr_sem.at[s],
                                            device_id=dev(first + kk, par), device_id_type=MESH)

    def slot(n):
        return lax.rem(n, GROUPS) * group

    def keeps(n, kk):
        return both(step(n)[1] + kk == e, par == c)

    def project(n):
        arrived(wv.at[pl.ds(3 * n, 3)], w_sem.at[n])

        @pl.when(n + 3 < steps)
        def _():
            for t in range(3):
                w_copy(n + 3, t).start()

        q, k, v = (jnp.dot(xv[...], wv[3 * n + t], preferred_element_type=F32) for t in range(3))
        s, at = lax.div(n, GROUPS), slot(n)
        for p in range(group // 2):
            sl = slice(128 * p, 128 * p + 128)
            q_lo, q_hi = q[:rows, sl], q[rows:, sl]
            stage[s, at + 2 * p, 0:rows] = jnp.where(low_q, q_lo, pltpu.roll(q_hi, hd, 1)).astype(BF16)
            stage[s, at + 2 * p + 1, 0:rows] = jnp.where(low_q, pltpu.roll(q_lo, hd, 1), q_hi).astype(BF16)
            stage[s, at + 2 * p, rows:] = jnp.where(low, k[:, sl], pltpu.roll(v[:, sl], hd, 1)).astype(BF16)
            stage[s, at + 2 * p + 1, rows:] = jnp.where(low, pltpu.roll(k[:, sl], hd, 1), v[:, sl]).astype(BF16)
        for m in range(1, group):
            qkv_send(n, lax.rem(xx + m, group)).start()
        own = lax.rem(xx, group)

        @pl.when(keeps(n, own))
        def _():
            buf[s, par, pair] = stage[s, at + own]

        @pl.when(jnp.logical_not(keeps(n, own)))
        def _():
            qkv_send(n, own).start()

    local = both(lax.div(e, half) == c, par == c)

    def of(ref, count, less):
        def wait(sem):
            @pl.when(less)
            def _():
                arrived(ref.at[pl.ds(0, count - 1)], sem)

            @pl.when(jnp.logical_not(less))
            def _():
                arrived(ref, sem)
        return wait

    def fwd(s, core):
        part = buf.at[s, core, :, pl.ds(rows, kv_rows)]
        return pltpu.make_async_remote_copy(part, part, fs_sem.at[s], fr_sem.at[s],
                                            device_id=dev(e, 1 - c), device_id_type=MESH)

    def forward(s):
        of(buf.at[s, c], half, local)(qr_sem.at[s])
        fwd(s, c).start()

    def o_send(s, u):
        return pltpu.make_async_remote_copy(ostage.at[s, u], obuf.at[s, e], os_sem.at[s], or_sem.at[s],
                                            device_id=dev(2 * lax.div(u, 2) + c, lax.rem(u, 2)), device_id_type=MESH)

    own_u = 2 * pair + c
    part_u = chips // BLOCKS

    def attend(s, b):
        qs = []
        for n in range(half // BLOCKS):
            qq = buf[s, c, b * (half // BLOCKS) + n, 0:rows].astype(F32)
            qs.append(jnp.where(low_q, qq, 0.0).astype(BF16))
            qs.append(jnp.where(low_q, pltpu.roll(qq, hd, 1), 0.0).astype(BF16))
        q = jnp.concatenate(qs, axis=0)
        m = den = o = None
        for side in range(2):
            kv = jnp.concatenate([buf[s, side, n, rows:] for n in range(half)], axis=0)
            logits = lax.dot_general(q, kv, (((1,), (1,)), ((), ())), preferred_element_type=F32)
            top = jnp.max(logits, axis=1, keepdims=True)
            new = top if side == 0 else jnp.maximum(m, top)
            w = jnp.exp2((logits - new) * scale)
            part = jnp.sum(w, axis=1, keepdims=True)
            wkv = jnp.dot(w.astype(BF16), kv, preferred_element_type=F32)
            if side == 0:
                m, den, o = new, part, wkv
            else:
                old = jnp.exp2((m - new) * scale)
                den = den * old + part
                o = (o * old + wkv) / den
        hr = rows // 2
        for u in range(part_u):
            lo, hi = o[u * rows:u * rows + hr], o[u * rows + hr:(u + 1) * rows]
            ostage[s, b * part_u + u] = jnp.where(low_o, pltpu.roll(lo, hd, 1), hi).astype(BF16)
        first = b * part_u + lax.rem(own_u, part_u)
        stays = both(first == own_u, par == c)
        for k in range(1, part_u):
            o_send(s, b * part_u + lax.rem(own_u + k, part_u)).start()

        @pl.when(stays)
        def _():
            obuf[s, e] = ostage[s, own_u]

        @pl.when(jnp.logical_not(stays))
        def _():
            o_send(s, first).start()

    def output(s):
        of(obuf.at[s], chips, par == c)(or_sem.at[s])
        tiles = []
        for p in range(half):
            a, b = obuf[s, 2 * p].astype(F32), obuf[s, 2 * p + 1].astype(F32)
            top = jnp.where(low_o, a, pltpu.roll(b, hd, 1))
            bot = jnp.where(low_o, pltpu.roll(a, hd, 1), b)
            tiles.append(jnp.concatenate([top, bot], axis=0).astype(BF16))
        o = jnp.concatenate(tiles, axis=1)
        arrived(wv.at[pl.ds(s * (o_parts // per), o_parts // per)], wo_sem.at[s])
        for n in range(o_parts):
            acc[:, n * o_cols:(n + 1) * o_cols] += jnp.dot(o, wo_part(s, n)[...], preferred_element_type=F32)

    def project_loop(n, _):
        project(n)
        return 0

    lax.fori_loop(0, steps, project_loop, 0)
    for s in range(chunks):
        for n in range(o_parts):
            wo_copy(s, n).start()
    acc[...] = jnp.zeros_like(acc)

    forward(0)

    def block_loop(n, _):
        s, b = lax.div(n, BLOCKS), lax.rem(n, BLOCKS)

        @pl.when(b == 0)
        def _():
            fwd(s, 1 - c).wait_recv()

        attend(s, b)

        @pl.when(both(b == 0, s + 1 < chunks))
        def _():
            forward(s + 1)

        @pl.when(both(b == BLOCKS - 1, s > 0))
        def _():
            output(s - 1)
        return 0

    lax.fori_loop(0, chunks * BLOCKS, block_loop, 0)
    output(chunks - 1)
    y_ref[...] = acc[...].astype(BF16)

    for s in range(chunks):
        of(stage.at[s], half, local)(qs_sem.at[s])
        fwd(s, c).wait_send()
        of(ostage.at[s], chips, par == c)(os_sem.at[s])


def solution(mesh):
    n_cx, n_cy = mesh.shape["cx"], mesh.shape["cy"]
    chips = n_cx * n_cy // 2

    def attend_local(x_blk, w_qkv, w_o):
        heads, hd, width = w_o.shape
        rows = x_blk.shape[1]
        chunks = heads // chips
        half = chips // 2
        group = half // GROUPS
        steps = chunks * GROUPS
        dma, vm = pltpu.SemaphoreType.DMA, pltpu.VMEM
        y = pl.pallas_call(
            functools.partial(kernel, (n_cx, n_cy, chips, chunks, heads, hd)),
            out_shape=pltpu.VMEM((rows, width), BF16),
            in_specs=[pl.BlockSpec(memory_space=pltpu.HBM)] * 3,
            out_specs=pl.BlockSpec(memory_space=pltpu.VMEM),
            scratch_shapes=[
                vm((2 * rows, width), BF16),
                vm((3 * steps, width, group * hd), BF16),
                vm((chunks, half, 3 * rows, 128), BF16),
                vm((chunks, 2, half, 3 * rows, 128), BF16),
                vm((chunks, chips, rows // 2, 128), BF16),
                vm((chunks, chips, rows // 2, 128), BF16),
                vm((rows, width), F32),
                dma, dma((steps,)), dma((chunks,)), dma, dma,
                dma((chunks,)), dma((chunks,)), dma((chunks,)), dma((chunks,)), dma((chunks,)), dma((chunks,)),
            ],
            compiler_params=pltpu.CompilerParams(
                collective_id=0, has_side_effects=True, vmem_limit_bytes=56 * 2 ** 20),
        )(x_blk[0], w_qkv, w_o.reshape(heads * hd, width))
        return y[None]

    return jax.shard_map(
        attend_local, mesh=mesh,
        in_specs=(P("dp", ("cx", "cy"), None), P(None, None), P(None, None, None)),
        out_specs=P("dp", ("cx", "cy"), None), check_vma=False)
```

time: 170 us -> 42.2 us (0.25)
  matrix products: 47 us -> 0 us
  Pallas kernels: 0 us -> 41.4 us
  waiting for transfers between devices: 37.8 us -> 0 us
  blocking collectives: 35.3 us -> 0 us
  local copies, waits for them, and re-layouts: 30.7 us -> 0.75 us
  between operations: 13.5 us -> 0.01 us
  other arithmetic: 4.88 us -> 0 us
    dot_general x4 -> x0, matrix products: 47 us -> none  [the longest x1 21.9 us: attend_local(): jnp.dot(x_blk[0], w_qkv, preferred_element_type=jnp.float32)]
    pallas_call x0 -> x1, Pallas kernels: none -> 41.4 us  [attend_local(): pl.pallas_call(functools.partial(kernel, (n_cx, n_cy, chips, chunks, head...]
    all_gather x1 -> x0, waiting for transfers between devices: 37.8 us -> none  [attend_local(): kv_all = lax.all_gather(qkv_rows[:, 1:], 'cx', axis=0, tiled=True)]
    all_to_all x2 -> x0, blocking collectives: 35.3 us -> none  [the longest x1 22.3 us: attend_local(): lax.all_to_all(qkv_rows.reshape(tok_rows, 3, num_heads, head_dim), 'cy',...]
    unnamed x12 -> x1, local copies, waits for them, and re-layouts: 17.5 us -> 0.75 us
    all_to_all x3 -> x0, local copies, waits for them, and re-layouts: 6.32 us -> none  [the longest x2 6.12 us: attend_local(): lax.all_to_all(qkv_rows.reshape(tok_rows, 3, num_heads, head_dim), 'cy',...]
    reshape x2 -> x0, local copies, waits for them, and re-layouts: 5.06 us -> none  [attend_local(): qkv_rows.reshape(tok_rows, 3, num_heads, head_dim)]
    reduce_sum x1 -> x0, other arithmetic: 4.88 us -> none  [attend_local(): row_sum = jnp.sum(weights, axis=-1, keepdims=True)]
  transfers between devices with their start and end apart: 1 -> 0, of which waited for: 1 -> 0; matrix products, arithmetic and copies ran while one was open for 0% -> 0% of each run, Pallas kernels for 0% -> 0%
where the time goes in v3:
time: 42.2 us
  Pallas kernels  41.4 us (98%)
  local copies, waits for them, and re-layouts  0.75 us (2%)
    pallas_call x1, Pallas kernels, attend_local(): pl.pallas_call(functools.partial(kernel, (n_cx, n_cy, chips, chunks, head...  41.4 us

profile of v3, /device:TPU:97, one launch (start us, length us, event | category | flops | bytes accessed | tf_op | source)
XLA Modules:
  0.0 42.2 jit_solution(16365009846416089303)
XLA Ops:
  0.0 41.4 %shard_map.37 = bf16[64,3072]{1,0:T(8,128)(2,1)S(1)} custom-call(bf16[64,3072]{1,0:T(8,128)(2,1)} %bitcast.5, bf16[3072,9216]{1,0:T(8,128)(2,1)} %w_ref.1, bf16[3072,3072]{1,0:T(8,128)(2,1)} %bitcast.4), custom_call_target="tpu_custom_call" | custom-call | tf_op jit(solution)/shard_map/pallas_call | solution.py:273
  41.4 0.7 %copy.5 = bf16[1,64,3072]{2,1,0:T(8,128)(2,1)} copy(bf16[1,64,3072]{2,1,0:T(8,128)(2,1)S(1)} %bitcast.3) | data formatting | bytes 786432

commit v4 on v3

--- a/solution.py
+++ b/solution.py
@@ -11,7 +11,8 @@
 BF16, F32 = jnp.bfloat16, jnp.float32
 LOG2E = 1.4426950408889634
 GROUPS = 2
-BLOCKS = 2
+KEY_PARTS = 2
+ORDER = (1, 3, 2)
 
 
 def both(a, b):
@@ -68,9 +69,6 @@
     def arrived(ref, sem):
         pltpu.make_async_copy(ref, ref, sem).wait()
 
-    for t in range(3):
-        w_copy(0, t).start()
-
     n_dev = n_cx * n_cy
     barrier = pltpu.get_barrier_semaphore()
 
@@ -80,7 +78,10 @@
                             device_id_type=MESH)
         return 0
 
-    lax.fori_loop(1, n_dev, greet, 0)
+    lax.fori_loop(1, n_dev // 2, greet, 0)
+    for t in range(3):
+        w_copy(0, t).start()
+    lax.fori_loop(n_dev // 2, n_dev, greet, 0)
     for t in range(3):
         w_copy(1, t).start()
     pl.semaphore_wait(barrier, n_dev - 1)
@@ -125,7 +126,7 @@
             stage[s, at + 2 * p + 1, 0:rows] = jnp.where(low_q, pltpu.roll(q_lo, hd, 1), q_hi).astype(BF16)
             stage[s, at + 2 * p, rows:] = jnp.where(low, k[:, sl], pltpu.roll(v[:, sl], hd, 1)).astype(BF16)
             stage[s, at + 2 * p + 1, rows:] = jnp.where(low, pltpu.roll(k[:, sl], hd, 1), v[:, sl]).astype(BF16)
-        for m in range(1, group):
+        for m in ORDER:
             qkv_send(n, lax.rem(xx + m, group)).start()
         own = lax.rem(xx, group)
 
@@ -164,48 +165,52 @@
                                             device_id=dev(2 * lax.div(u, 2) + c, lax.rem(u, 2)), device_id_type=MESH)
 
     own_u = 2 * pair + c
-    part_u = chips // BLOCKS
-
-    def attend(s, b):
+    key_chips = half // KEY_PARTS
+
+    def attend(s):
         qs = []
-        for n in range(half // BLOCKS):
-            qq = buf[s, c, b * (half // BLOCKS) + n, 0:rows].astype(F32)
+        for n in range(half):
+            qq = buf[s, c, n, 0:rows].astype(F32)
             qs.append(jnp.where(low_q, qq, 0.0).astype(BF16))
             qs.append(jnp.where(low_q, pltpu.roll(qq, hd, 1), 0.0).astype(BF16))
         q = jnp.concatenate(qs, axis=0)
         m = den = o = None
         for side in range(2):
-            kv = jnp.concatenate([buf[s, side, n, rows:] for n in range(half)], axis=0)
-            logits = lax.dot_general(q, kv, (((1,), (1,)), ((), ())), preferred_element_type=F32)
-            top = jnp.max(logits, axis=1, keepdims=True)
-            new = top if side == 0 else jnp.maximum(m, top)
-            w = jnp.exp2((logits - new) * scale)
-            part = jnp.sum(w, axis=1, keepdims=True)
-            wkv = jnp.dot(w.astype(BF16), kv, preferred_element_type=F32)
-            if side == 0:
-                m, den, o = new, part, wkv
-            else:
-                old = jnp.exp2((m - new) * scale)
-                den = den * old + part
-                o = (o * old + wkv) / den
+            core = c if side == 0 else 1 - c
+            if side == 1:
+                fwd(s, 1 - c).wait_recv()
+            for g in range(KEY_PARTS):
+                kv = jnp.concatenate([buf[s, core, g * key_chips + n, rows:] for n in range(key_chips)], axis=0)
+                logits = lax.dot_general(q, kv, (((1,), (1,)), ((), ())), preferred_element_type=F32)
+                top = jnp.max(logits, axis=1, keepdims=True)
+                new = top if m is None else jnp.maximum(m, top)
+                w = jnp.exp2((logits - new) * scale)
+                part = jnp.sum(w, axis=1, keepdims=True)
+                wkv = jnp.dot(w.astype(BF16), kv, preferred_element_type=F32)
+                if m is None:
+                    den, o = part, wkv
+                else:
+                    old = jnp.exp2((m - new) * scale)
+                    den, o = den * old + part, o * old + wkv
+                m = new
+        o = o / den
         hr = rows // 2
-        for u in range(part_u):
+        for u in range(chips):
             lo, hi = o[u * rows:u * rows + hr], o[u * rows + hr:(u + 1) * rows]
-            ostage[s, b * part_u + u] = jnp.where(low_o, pltpu.roll(lo, hd, 1), hi).astype(BF16)
-        first = b * part_u + lax.rem(own_u, part_u)
-        stays = both(first == own_u, par == c)
-        for k in range(1, part_u):
-            o_send(s, b * part_u + lax.rem(own_u + k, part_u)).start()
-
-        @pl.when(stays)
+            ostage[s, u] = jnp.where(low_o, pltpu.roll(lo, hd, 1), hi).astype(BF16)
+
+        for k in range(1, chips):
+            o_send(s, lax.rem(own_u + k, chips)).start()
+
+        @pl.when(par == c)
         def _():
             obuf[s, e] = ostage[s, own_u]
 
-        @pl.when(jnp.logical_not(stays))
-        def _():
-            o_send(s, first).start()
-
-    def output(s):
+        @pl.when(par != c)
+        def _():
+            o_send(s, own_u).start()
+
+    def output(s, last=False):
         of(obuf.at[s], chips, par == c)(or_sem.at[s])
         tiles = []
         for p in range(half):
@@ -216,7 +221,12 @@
         o = jnp.concatenate(tiles, axis=1)
         arrived(wv.at[pl.ds(s * (o_parts // per), o_parts // per)], wo_sem.at[s])
         for n in range(o_parts):
-            acc[:, n * o_cols:(n + 1) * o_cols] += jnp.dot(o, wo_part(s, n)[...], preferred_element_type=F32)
+            cols = slice(n * o_cols, (n + 1) * o_cols)
+            total = acc[:, cols] + jnp.dot(o, wo_part(s, n)[...], preferred_element_type=F32)
+            if last:
+                y_ref[:, cols] = total.astype(BF16)
+            else:
+                acc[:, cols] = total
 
     def project_loop(n, _):
         project(n)
@@ -228,29 +238,15 @@
             wo_copy(s, n).start()
     acc[...] = jnp.zeros_like(acc)
 
-    forward(0)
-
-    def block_loop(n, _):
-        s, b = lax.div(n, BLOCKS), lax.rem(n, BLOCKS)
-
-        @pl.when(b == 0)
-        def _():
-            fwd(s, 1 - c).wait_recv()
-
-        attend(s, b)
-
-        @pl.when(both(b == 0, s + 1 < chunks))
-        def _():
-            forward(s + 1)
-
-        @pl.when(both(b == BLOCKS - 1, s > 0))
-        def _():
-            output(s - 1)
+    def chunk_loop(s, _):
+        forward(s)
+        attend(s)
         return 0
 
-    lax.fori_loop(0, chunks * BLOCKS, block_loop, 0)
-    output(chunks - 1)
-    y_ref[...] = acc[...].astype(BF16)
+    lax.fori_loop(0, chunks, chunk_loop, 0)
+    for s in range(chunks - 1):
+        output(s)
+    output(chunks - 1, last=True)
 
     for s in range(chunks):
         of(stage.at[s], half, local)(qs_sem.at[s])

time: 42.2 us -> 39.4 us (0.934)
  Pallas kernels: 41.4 us -> 38.5 us
    pallas_call x1, Pallas kernels: 41.4 us -> 38.5 us  [attend_local(): pl.pallas_call(functools.partial(kernel, (n_cx, n_cy, chips, chunks, head...]
where the time goes in v4:
time: 39.4 us; the launch traced here: 39.3 us
  Pallas kernels  38.5 us (98%)
  local copies, waits for them, and re-layouts  0.75 us (2%)
    pallas_call x1, Pallas kernels, attend_local(): pl.pallas_call(functools.partial(kernel, (n_cx, n_cy, chips, chunks, head...  38.5 us

profile of v4, /device:TPU:97, one launch (start us, length us, event | category | flops | bytes accessed | tf_op | source)
XLA Modules:
  0.0 39.3 jit_solution(6245116619353003832)
XLA Ops:
  0.0 38.5 %shard_map.37 = bf16[64,3072]{1,0:T(8,128)(2,1)S(1)} custom-call(bf16[64,3072]{1,0:T(8,128)(2,1)} %bitcast.5, bf16[3072,9216]{1,0:T(8,128)(2,1)} %w_ref.1, bf16[3072,3072]{1,0:T(8,128)(2,1)} %bitcast.4), custom_call_target="tpu_custom_call" | custom-call | tf_op jit(solution)/shard_map/pallas_call | solution.py:269
  38.5 0.7 %copy.5 = bf16[1,64,3072]{2,1,0:T(8,128)(2,1)} copy(bf16[1,64,3072]{2,1,0:T(8,128)(2,1)S(1)} %bitcast.3) | data formatting | bytes 786432

commit v5 on v4

--- a/solution.py
+++ b/solution.py
@@ -25,7 +25,6 @@
     row_chips = n_cy // 2
     half = chips // 2
     rows, width = x_ref.shape
-    kv_rows = 2 * rows
     span = half * hd
     scale = hd ** -0.5 * LOG2E
     group = half // GROUPS
@@ -66,6 +65,10 @@
         src = wo_ref.at[pl.ds(pl.multiple_of(s * o_rows, o_rows), o_rows), pl.ds(n * o_cols, o_cols)]
         return pltpu.make_async_copy(src, wo_part(s, n), wo_sem.at[s])
 
+    def w_start(n):
+        for t in range(3):
+            w_copy(n, t).start()
+
     def arrived(ref, sem):
         pltpu.make_async_copy(ref, ref, sem).wait()
 
@@ -79,64 +82,87 @@
         return 0
 
     lax.fori_loop(1, n_dev // 2, greet, 0)
-    for t in range(3):
-        w_copy(0, t).start()
+    w_start(0)
     lax.fori_loop(n_dev // 2, n_dev, greet, 0)
-    for t in range(3):
-        w_copy(1, t).start()
+    w_start(1)
+
+    low = lax.broadcasted_iota(jnp.int32, (rows, 128), 1) < hd
+    low_o = low[:rows // 2]
+    q_rows = rows // 2
+
+    def slot(n):
+        return lax.rem(n, GROUPS) * group
+
+    def keeps(n, kk):
+        return both(step(n)[1] + kk == e, par == c)
+
+    def qkv_send(n, kk, r=None):
+        s, first = step(n)
+        src, dst = stage.at[s, slot(n) + kk], buf.at[s, par, pair]
+        if r is not None:
+            src, dst = src.at[r], dst.at[r]
+        return pltpu.make_async_remote_copy(src, dst, qs_sem.at[s], qr_sem.at[s],
+                                            device_id=dev(first + kk, par), device_id_type=MESH)
+
+    def send(n, r=None):
+        for m in ORDER:
+            qkv_send(n, lax.rem(xx + m, group), r).start()
+        own = lax.rem(xx, group)
+        s = lax.div(n, GROUPS)
+
+        @pl.when(keeps(n, own))
+        def _():
+            if r is None:
+                buf[s, par, pair] = stage[s, slot(n) + own]
+            else:
+                buf[s, par, pair, r] = stage[s, slot(n) + own, r]
+
+        @pl.when(jnp.logical_not(keeps(n, own)))
+        def _():
+            qkv_send(n, own, r).start()
+
+    def pack(n, r, q, k, v):
+        s, at = lax.div(n, GROUPS), slot(n)
+        for p in range(group // 2):
+            sl = slice(128 * p, 128 * p + 128)
+            top, bot, kk, vv = q[:q_rows, sl], q[q_rows:, sl], k[:, sl], v[:, sl]
+            stage[s, at + 2 * p, r, 0:q_rows] = jnp.where(low_o, top, pltpu.roll(bot, hd, 1)).astype(BF16)
+            stage[s, at + 2 * p + 1, r, 0:q_rows] = jnp.where(low_o, pltpu.roll(top, hd, 1), bot).astype(BF16)
+            stage[s, at + 2 * p, r, q_rows:] = jnp.where(low, kk, pltpu.roll(vv, hd, 1)).astype(BF16)
+            stage[s, at + 2 * p + 1, r, q_rows:] = jnp.where(low, pltpu.roll(kk, hd, 1), vv).astype(BF16)
+
+    def project_half(n, r):
+        x_half = xv[pl.ds(pl.multiple_of(r * rows, rows), rows)]
+        pack(n, r, *(jnp.dot(x_half, wv[3 * n + t], preferred_element_type=F32) for t in range(3)))
+
+    def project(n):
+        arrived(wv.at[pl.ds(3 * n, 3)], w_sem.at[n])
+        q, k, v = (jnp.dot(xv[...], wv[3 * n + t], preferred_element_type=F32) for t in range(3))
+        for r in range(2):
+            half_rows = slice(r * rows, (r + 1) * rows)
+            pack(n, r, q[half_rows], k[half_rows], v[half_rows])
+        send(n)
+
+    x_in.wait()
+    arrived(wv.at[pl.ds(0, 3)], w_sem.at[0])
+    w_start(2)
+    w_start(3)
+    project_half(0, c)
     pl.semaphore_wait(barrier, n_dev - 1)
-
-    x_in.wait()
-    for t in range(3):
-        w_copy(2, t).start()
     x_swap = pltpu.make_async_remote_copy(xv.at[my_rows], xv.at[my_rows], xs_sem, xr_sem,
                                           device_id=dev(e, 1 - c), device_id_type=MESH)
     x_swap.start()
+    send(0, c)
+    for n in range(1, GROUPS):
+        arrived(wv.at[pl.ds(3 * n, 3)], w_sem.at[n])
+        for m in range(n + 3, min(steps, GROUPS + n + 3)):
+            w_start(m)
+        project_half(n, c)
+        send(n, c)
     x_swap.wait()
-
-    low = lax.broadcasted_iota(jnp.int32, (kv_rows, 128), 1) < hd
-    low_q = low[:rows]
-    low_o = low[:rows // 2]
-
-    def qkv_send(n, kk):
-        s, first = step(n)
-        return pltpu.make_async_remote_copy(stage.at[s, slot(n) + kk], buf.at[s, par, pair], qs_sem.at[s], qr_sem.at[s],
-                                            device_id=dev(first + kk, par), device_id_type=MESH)
-
-    def slot(n):
-        return lax.rem(n, GROUPS) * group
-
-    def keeps(n, kk):
-        return both(step(n)[1] + kk == e, par == c)
-
-    def project(n):
-        arrived(wv.at[pl.ds(3 * n, 3)], w_sem.at[n])
-
-        @pl.when(n + 3 < steps)
-        def _():
-            for t in range(3):
-                w_copy(n + 3, t).start()
-
-        q, k, v = (jnp.dot(xv[...], wv[3 * n + t], preferred_element_type=F32) for t in range(3))
-        s, at = lax.div(n, GROUPS), slot(n)
-        for p in range(group // 2):
-            sl = slice(128 * p, 128 * p + 128)
-            q_lo, q_hi = q[:rows, sl], q[rows:, sl]
-            stage[s, at + 2 * p, 0:rows] = jnp.where(low_q, q_lo, pltpu.roll(q_hi, hd, 1)).astype(BF16)
-            stage[s, at + 2 * p + 1, 0:rows] = jnp.where(low_q, pltpu.roll(q_lo, hd, 1), q_hi).astype(BF16)
-            stage[s, at + 2 * p, rows:] = jnp.where(low, k[:, sl], pltpu.roll(v[:, sl], hd, 1)).astype(BF16)
-            stage[s, at + 2 * p + 1, rows:] = jnp.where(low, pltpu.roll(k[:, sl], hd, 1), v[:, sl]).astype(BF16)
-        for m in ORDER:
-            qkv_send(n, lax.rem(xx + m, group)).start()
-        own = lax.rem(xx, group)
-
-        @pl.when(keeps(n, own))
-        def _():
-            buf[s, par, pair] = stage[s, at + own]
-
-        @pl.when(jnp.logical_not(keeps(n, own)))
-        def _():
-            qkv_send(n, own).start()
+    for n in range(GROUPS):
+        project_half(n, 1 - c)
+        send(n, 1 - c)
 
     local = both(lax.div(e, half) == c, par == c)
 
@@ -152,7 +178,7 @@
         return wait
 
     def fwd(s, core):
-        part = buf.at[s, core, :, pl.ds(rows, kv_rows)]
+        part = buf.at[s, core, :, :, pl.ds(q_rows, rows)]
         return pltpu.make_async_remote_copy(part, part, fs_sem.at[s], fr_sem.at[s],
                                             device_id=dev(e, 1 - c), device_id_type=MESH)
 
@@ -170,9 +196,10 @@
     def attend(s):
         qs = []
         for n in range(half):
-            qq = buf[s, c, n, 0:rows].astype(F32)
-            qs.append(jnp.where(low_q, qq, 0.0).astype(BF16))
-            qs.append(jnp.where(low_q, pltpu.roll(qq, hd, 1), 0.0).astype(BF16))
+            for r in range(2):
+                qq = buf[s, c, n, r, 0:q_rows].astype(F32)
+                qs.append(jnp.where(low_o, qq, 0.0).astype(BF16))
+                qs.append(jnp.where(low_o, pltpu.roll(qq, hd, 1), 0.0).astype(BF16))
         q = jnp.concatenate(qs, axis=0)
         m = den = o = None
         for side in range(2):
@@ -180,7 +207,8 @@
             if side == 1:
                 fwd(s, 1 - c).wait_recv()
             for g in range(KEY_PARTS):
-                kv = jnp.concatenate([buf[s, core, g * key_chips + n, rows:] for n in range(key_chips)], axis=0)
+                kv = jnp.concatenate([buf[s, core, g * key_chips + n, r, q_rows:]
+                                      for n in range(key_chips) for r in range(2)], axis=0)
                 logits = lax.dot_general(q, kv, (((1,), (1,)), ((), ())), preferred_element_type=F32)
                 top = jnp.max(logits, axis=1, keepdims=True)
                 new = top if m is None else jnp.maximum(m, top)
@@ -232,7 +260,7 @@
         project(n)
         return 0
 
-    lax.fori_loop(0, steps, project_loop, 0)
+    lax.fori_loop(GROUPS, steps, project_loop, 0)
     for s in range(chunks):
         for n in range(o_parts):
             wo_copy(s, n).start()
@@ -274,8 +302,8 @@
             scratch_shapes=[
                 vm((2 * rows, width), BF16),
                 vm((3 * steps, width, group * hd), BF16),
-                vm((chunks, half, 3 * rows, 128), BF16),
-                vm((chunks, 2, half, 3 * rows, 128), BF16),
+                vm((chunks, half, 2, 3 * rows // 2, 128), BF16),
+                vm((chunks, 2, half, 2, 3 * rows // 2, 128), BF16),
                 vm((chunks, chips, rows // 2, 128), BF16),
                 vm((chunks, chips, rows // 2, 128), BF16),
                 vm((rows, width), F32),

time: 39.4 us -> 38.7 us (0.982)
  Pallas kernels: 38.5 us -> 37.9 us
    pallas_call x1, Pallas kernels: 38.5 us -> 37.9 us  [attend_local(): pl.pallas_call(functools.partial(kernel, (n_cx, n_cy, chips, chunks, head...]
where the time goes in v5:
time: 38.7 us
  Pallas kernels  37.9 us (98%)
  local copies, waits for them, and re-layouts  0.75 us (2%)
    pallas_call x1, Pallas kernels, attend_local(): pl.pallas_call(functools.partial(kernel, (n_cx, n_cy, chips, chunks, head...  37.9 us

profile of v5, /device:TPU:97, one launch (start us, length us, event | category | flops | bytes accessed | tf_op | source)
XLA Modules:
  0.0 38.7 jit_solution(13829105796376406593)
XLA Ops:
  0.0 37.9 %shard_map.37 = bf16[64,3072]{1,0:T(8,128)(2,1)S(1)} custom-call(bf16[64,3072]{1,0:T(8,128)(2,1)} %bitcast.5, bf16[3072,9216]{1,0:T(8,128)(2,1)} %w_ref.1, bf16[3072,3072]{1,0:T(8,128)(2,1)} %bitcast.4), custom_call_target="tpu_custom_call" | custom-call | tf_op jit(solution)/shard_map/pallas_call | solution.py:297
  37.9 0.7 %copy.5 = bf16[1,64,3072]{2,1,0:T(8,128)(2,1)} copy(bf16[1,64,3072]{2,1,0:T(8,128)(2,1)S(1)} %bitcast.3) | data formatting | bytes 786432

commit v6 on v5

--- a/solution.py
+++ b/solution.py
@@ -186,11 +186,6 @@
         of(buf.at[s, c], half, local)(qr_sem.at[s])
         fwd(s, c).start()
 
-    def o_send(s, u):
-        return pltpu.make_async_remote_copy(ostage.at[s, u], obuf.at[s, e], os_sem.at[s], or_sem.at[s],
-                                            device_id=dev(2 * lax.div(u, 2) + c, lax.rem(u, 2)), device_id_type=MESH)
-
-    own_u = 2 * pair + c
     key_chips = half // KEY_PARTS
 
     def attend(s):
@@ -227,34 +222,47 @@
             lo, hi = o[u * rows:u * rows + hr], o[u * rows + hr:(u + 1) * rows]
             ostage[s, u] = jnp.where(low_o, pltpu.roll(lo, hd, 1), hi).astype(BF16)
 
-        for k in range(1, chips):
-            o_send(s, lax.rem(own_u + k, chips)).start()
-
-        @pl.when(par == c)
-        def _():
-            obuf[s, e] = ostage[s, own_u]
-
-        @pl.when(par != c)
-        def _():
-            o_send(s, own_u).start()
+        cols = row_chips // 2
+        for dy in list(range(1, n_cx)) + [0]:
+            row = lax.rem(i + dy, n_cx)
+            for m in range(2 * cols):
+                col, core = m // 2, m % 2
+                u = row * 2 * cols + m
+                copy = pltpu.make_async_remote_copy(
+                    ostage.at[s, u], obuf.at[s, e], os_sem.at[s], or_sem.at[s, lax.div(e, half)],
+                    device_id={"cx": row, "cy": 4 * col + 2 * c + core}, device_id_type=MESH)
+                if dy:
+                    copy.start()
+                    continue
+                stays = both(both(col == lax.div(xx, 2), par == c), core == c)
+
+                @pl.when(stays)
+                def _():
+                    obuf[s, e] = ostage[s, u]
+
+                @pl.when(jnp.logical_not(stays))
+                def _():
+                    copy.start()
 
     def output(s, last=False):
-        of(obuf.at[s], chips, par == c)(or_sem.at[s])
-        tiles = []
-        for p in range(half):
-            a, b = obuf[s, 2 * p].astype(F32), obuf[s, 2 * p + 1].astype(F32)
-            top = jnp.where(low_o, a, pltpu.roll(b, hd, 1))
-            bot = jnp.where(low_o, pltpu.roll(a, hd, 1), b)
-            tiles.append(jnp.concatenate([top, bot], axis=0).astype(BF16))
-        o = jnp.concatenate(tiles, axis=1)
         arrived(wv.at[pl.ds(s * (o_parts // per), o_parts // per)], wo_sem.at[s])
-        for n in range(o_parts):
-            cols = slice(n * o_cols, (n + 1) * o_cols)
-            total = acc[:, cols] + jnp.dot(o, wo_part(s, n)[...], preferred_element_type=F32)
-            if last:
-                y_ref[:, cols] = total.astype(BF16)
-            else:
-                acc[:, cols] = total
+        for h in range(2):
+            of(obuf.at[s, pl.ds(h * half, half)], half, both(par == c, lax.div(e, half) == h))(or_sem.at[s, h])
+            tiles = []
+            for p in range(half // 2):
+                a, b = (obuf[s, h * half + 2 * p + q].astype(F32) for q in range(2))
+                top = jnp.where(low_o, a, pltpu.roll(b, hd, 1))
+                bot = jnp.where(low_o, pltpu.roll(a, hd, 1), b)
+                tiles.append(jnp.concatenate([top, bot], axis=0).astype(BF16))
+            o = jnp.concatenate(tiles, axis=1)
+            depth = slice(h * half * hd, (h + 1) * half * hd)
+            for n in range(o_parts):
+                cols = slice(n * o_cols, (n + 1) * o_cols)
+                total = acc[:, cols] + jnp.dot(o, wo_part(s, n)[depth], preferred_element_type=F32)
+                if last and h:
+                    y_ref[:, cols] = total.astype(BF16)
+                else:
+                    acc[:, cols] = total
 
     def project_loop(n, _):
         project(n)
@@ -308,7 +316,7 @@
                 vm((chunks, chips, rows // 2, 128), BF16),
                 vm((rows, width), F32),
                 dma, dma((steps,)), dma((chunks,)), dma, dma,
-                dma((chunks,)), dma((chunks,)), dma((chunks,)), dma((chunks,)), dma((chunks,)), dma((chunks,)),
+                dma((chunks,)), dma((chunks,)), dma((chunks,)), dma((chunks,)), dma((chunks,)), dma((chunks, 2)),
             ],
             compiler_params=pltpu.CompilerParams(
                 collective_id=0, has_side_effects=True, vmem_limit_bytes=56 * 2 ** 20),

time: 38.7 us -> 38 us (0.982)
  Pallas kernels: 37.9 us -> 37.1 us
    pallas_call x1, Pallas kernels: 37.9 us -> 37.1 us  [attend_local(): pl.pallas_call(functools.partial(kernel, (n_cx, n_cy, chips, chunks, head...]
where the time goes in v6:
time: 38 us; the launch traced here: 37.9 us
  Pallas kernels  37.1 us (98%)
  local copies, waits for them, and re-layouts  0.75 us (2%)
    pallas_call x1, Pallas kernels, attend_local(): pl.pallas_call(functools.partial(kernel, (n_cx, n_cy, chips, chunks, head...  37.1 us

profile of v6, /device:TPU:97, one launch (start us, length us, event | category | flops | bytes accessed | tf_op | source)
XLA Modules:
  0.0 37.9 jit_solution(17743559983822701284)
XLA Ops:
  0.0 37.1 %shard_map.37 = bf16[64,3072]{1,0:T(8,128)(2,1)S(1)} custom-call(bf16[64,3072]{1,0:T(8,128)(2,1)} %bitcast.5, bf16[3072,9216]{1,0:T(8,128)(2,1)} %w_ref.1, bf16[3072,3072]{1,0:T(8,128)(2,1)} %bitcast.4), custom_call_target="tpu_custom_call" | custom-call | tf_op jit(solution)/shard_map/pallas_call | solution.py:305
  37.2 0.7 %copy.5 = bf16[1,64,3072]{2,1,0:T(8,128)(2,1)} copy(bf16[1,64,3072]{2,1,0:T(8,128)(2,1)S(1)} %bitcast.3) | data formatting | bytes 786432

commit v7 on v6

--- a/solution.py
+++ b/solution.py
@@ -102,7 +102,8 @@
         if r is not None:
             src, dst = src.at[r], dst.at[r]
         return pltpu.make_async_remote_copy(src, dst, qs_sem.at[s], qr_sem.at[s],
-                                            device_id=dev(first + kk, par), device_id_type=MESH)
+                                            device_id={"cx": lax.div(first, row_chips), "cy": 2 * kk + par},
+                                            device_id_type=MESH)
 
     def send(n, r=None):
         for m in ORDER:
@@ -300,6 +301,7 @@
         chunks = heads // chips
         half = chips // 2
         group = half // GROUPS
+        assert group == n_cy // 2
         steps = chunks * GROUPS
         dma, vm = pltpu.SemaphoreType.DMA, pltpu.VMEM
         y = pl.pallas_call(

time: 38 us -> 37.6 us (0.989)
  no operation moved by 1% of the time
where the time goes in v7:
time: 37.6 us; the launch traced here: 37.5 us
  Pallas kernels  36.8 us (98%)
  local copies, waits for them, and re-layouts  0.75 us (2%)
    pallas_call x1, Pallas kernels, attend_local(): pl.pallas_call(functools.partial(kernel, (n_cx, n_cy, chips, chunks, head...  36.8 us

profile of v7, /device:TPU:97, one launch (start us, length us, event | category | flops | bytes accessed | tf_op | source)
XLA Modules:
  0.0 37.5 jit_solution(1107700185035070361)
XLA Ops:
  0.0 36.8 %shard_map.37 = bf16[64,3072]{1,0:T(8,128)(2,1)S(1)} custom-call(bf16[64,3072]{1,0:T(8,128)(2,1)} %bitcast.5, bf16[3072,9216]{1,0:T(8,128)(2,1)} %w_ref.1, bf16[3072,3072]{1,0:T(8,128)(2,1)} %bitcast.4), custom_call_target="tpu_custom_call" | custom-call | tf_op jit(solution)/shard_map/pallas_call | solution.py:307
  36.8 0.7 %copy.5 = bf16[1,64,3072]{2,1,0:T(8,128)(2,1)} copy(bf16[1,64,3072]{2,1,0:T(8,128)(2,1)S(1)} %bitcast.3) | data formatting | bytes 786432
